TPU v7x, 32 devices: a whole 2x2x4 slice. The times are simulated.
32 devices in a mesh: row: 2 (over x), col: 4 (over z), depth: 4 (over y, core).
Axes of the slice: x: 2, y: 2, z: 4, core: 2. Of those that a mesh axis runs over, the one named last changes fastest.
Arguments:
- acts: bfloat16 [8192, 5120], P(('depth', 'col'), 'row'), may hold values from -6 to 6
- grad_out: bfloat16 [8192, 13824], P(('depth', 'row'), 'col'), may hold values from -6 to 6
- weight: bfloat16 [5120, 13824], P('row', 'col'), may hold values from -0.078125 to 0.078125
- master: float32 [5120, 13824], P(('row', 'depth'), 'col'), may hold values from -0.078125 to 0.078125
- moment_one: float32 [5120, 13824], P(('row', 'depth'), 'col'), may hold values from -4 to 4
- moment_two: float32 [5120, 13824], P(('row', 'depth'), 'col'), may hold values from 0.05 to 2
Outputs:
- grad_in: bfloat16 [8192, 5120], P(('depth', 'col'), 'row')
- new_weight: bfloat16 [5120, 13824], P('row', 'col')
- new_master: float32 [5120, 13824], P(('row', 'depth'), 'col')
- new_moment_one: float32 [5120, 13824], P(('row', 'depth'), 'col')
- new_moment_two: float32 [5120, 13824], P(('row', 'depth'), 'col')
All inputs are finite; a program needn't handle non-finite values.
Results may differ from a plain program's by a relative error of at most 0.0035.
Values may be sent and summed in bfloat16 or wider, within the bound.
A program may use at most 192 MiB of HBM per device.

v0:
```python
import math

import jax
import jax.numpy as jnp
from jax import lax
from jax.sharding import PartitionSpec as P

STEP = 10


def per_device(acts, grad_out, weight, master, moment_one, moment_two):
    whole_acts = lax.all_gather(acts, "col", axis=0, tiled=True)
    tokens_total = acts.shape[0] * lax.axis_size("col") * lax.axis_size("depth")
    whole_cotangent = lax.all_gather(grad_out, "row", axis=0, tiled=True)
    picked = whole_cotangent
    input_sum = lax.psum_scatter(
        lax.dot_general(
            picked, weight, (((1,), (1,)), ((), ())), preferred_element_type=jnp.float32
        ),
        "col",
        scatter_dimension=0,
        tiled=True,
    )
    picked = whole_acts
    grad_sum = lax.psum_scatter(
        lax.dot_general(
            picked, whole_cotangent, (((0,), (0,)), ((), ())), preferred_element_type=jnp.float32
        ).astype(jnp.bfloat16),
        "depth",
        scatter_dimension=0,
        tiled=True,
    ).astype(jnp.float32)
    grad_in = input_sum.astype(jnp.bfloat16)
    grad = grad_sum * jnp.float32(1.0 / math.sqrt(tokens_total))
    new_moment_one = 0.9 * moment_one + 0.1 * grad
    new_moment_two = 0.95 * moment_two + 0.05 * grad * grad
    first_fix = 1.0 - 0.9**STEP
    second_fix = 1.0 - 0.95**STEP
    update = new_moment_one / first_fix / (jnp.sqrt(new_moment_two / second_fix) + 1e-08)
    new_master = master - 0.01 * (update + 0.1 * master)
    new_weight = lax.all_gather(new_master.astype(jnp.bfloat16), "depth", axis=0, tiled=True)
    return (grad_in, new_weight, new_master, new_moment_one, new_moment_two)


def solution(mesh):
    placed = (
        P(("depth", "col"), "row"),
        P(("depth", "row"), "col"),
        P("row", "col"),
        P(("row", "depth"), "col"),
        P(("row", "depth"), "col"),
        P(("row", "depth"), "col"),
    )
    return jax.shard_map(
        per_device,
        mesh=mesh,
        in_specs=placed,
        out_specs=(
            P(("depth", "col"), "row"),
            P("row", "col"),
            P(("row", "depth"), "col"),
            P(("row", "depth"), "col"),
            P(("row", "depth"), "col"),
        ),
        check_vma=False,
    )
```

profile of v0, /device:TPU:0, one launch (start us, length us, event | category | flops | bytes accessed | tf_op | source)
XLA Modules:
  0.0 1031.1 jit_solution(5081694535935332860)
XLA Ops:
  7.2 0.0 all-gather.4.cloned.1.call-start
  7.2 0.7 all-gather.4.cloned.1.call-update
  7.9 0.0 all-gather.6.cloned.1.call-start
  7.9 0.7 all-gather.6.cloned.1.call-update
  8.6 0.0 reduce-scatter.5.cloned.1.call-start
  8.7 173.3 %all-gather.4.cloned.1.call-done = bf16[2048,3456]{1,0:T(8,128)(2,1)} async-done(((bf16[1024,3456]{1,0:T(8,128)(2,1)}), bf16[2048,3456]{1,0:T(8,128)(2,1)}) %all-gather.4.cloned.1.call-update) | async-done | bytes 14155792 | tf_op jit(solution)/shard_map/all_gather | solution.py:14
  182.0 185.5 %all-gather.6.cloned.1.call-done = bf16[2048,2560]{1,0:T(8,128)(2,1)} async-done(((bf16[512,2560]{1,0:T(8,128)(2,1)}), bf16[2048,2560]{1,0:T(8,128)(2,1)}) %all-gather.6.cloned.1.call-update) | async-done | bytes 10485776 | tf_op jit(solution)/shard_map/all_gather | solution.py:12
  367.5 45.6 %convolution_convert_fusion = bf16[2560,3456]{1,0:T(8,128)(2,1)} fusion(bf16[2048,2560]{1,0:T(8,128)(2,1)} %all-gather.6.cloned.1.call-done, bf16[2048,3456]{1,0:T(8,128)(2,1)} %all-gather.4.cloned.1.call-done), kind=kOutput, calls=%fused_computation | convolution fusion | flops 36247633920 | bytes 42336256 | tf_op jit(solution)/shard_map/dot_general | solution.py:26
  413.1 0.0 reduce-scatter.5.cloned.1.call-update
  413.2 0.0 reduce-scatter.3.cloned.1.call-start
  413.2 47.3 %fusion.6 = f32[2048,2560]{1,0:T(8,128)} fusion(bf16[2048,3456]{1,0:T(8,128)(2,1)} %all-gather.4.cloned.1.call-done, bf16[2560,3456]{1,0:T(8,128)(2,1)} %param.8), kind=kOutput, calls=%fused_computation.9 | convolution fusion | flops 36238786560 | bytes 52822016 | tf_op jit(solution)/shard_map/dot_general | solution.py:17
  460.5 0.0 reduce-scatter.3.cloned.1.call-update
  460.5 0.2 all-gather.8.cloned.1.call-start
  460.8 81.3 %reduce-scatter.5.cloned.1.call-done = bf16[640,3456]{1,0:T(8,128)(2,1)} async-done(((bf16[2560,3456]{1,0:T(8,128)(2,1)}), bf16[640,3456]{1,0:T(8,128)(2,1)}) %reduce-scatter.5.cloned.1.call-update) | async-done | bytes 4423696 | tf_op jit(solution)/shard_map/reduce_scatter | solution.py:25
  542.1 23.0 %fusion.3 = (bf16[640,3456]{1,0:T(8,128)(2,1)}, f32[640,3456]{1,0:T(8,128)}, f32[640,3456]{1,0:T(8,128)}, f32[640,3456]{1,0:T(8,128)}) fusion(f32[640,3456]{1,0:T(8,128)} %param.9, bf16[640,3456]{1,0:T(8,128)(2,1)} %reduce-scatter.5.cloned.1.call-done, f32[640,3456]{1,0:T(8,128)} %param.10, f32[640,3456]{1,0:T(8,128)} %param.11), kind=kLoop, calls=%fused_computation.8 | loop fusion | flops 39813120 | bytes 61931520 | tf_op jit(solution)/shard_map/convert_element_type | solution.py:41
  565.1 0.0 all-gather.8.cloned.1.call-update
  565.2 326.6 %reduce-scatter.3.cloned.1.call-done = f32[512,2560]{1,0:T(8,128)} async-done(((f32[2048,2560]{1,0:T(8,128)}), f32[512,2560]{1,0:T(8,128)}) %reduce-scatter.3.cloned.1.call-update) | async-done | bytes 5242896 | tf_op jit(solution)/shard_map/reduce_scatter | solution.py:16
  891.7 4.3 convert_element_type.12
  896.0 112.6 %all-gather.8.cloned.1.call-done = bf16[2560,3456]{1,0:T(8,128)(2,1)} async-done(((bf16[640,3456]{1,0:T(8,128)(2,1)}), bf16[2560,3456]{1,0:T(8,128)(2,1)}) %all-gather.8.cloned.1.call-update) | async-done | bytes 17694736 | tf_op jit(solution)/shard_map/all_gather | solution.py:41
  1008.6 16.0 %copy.12 = bf16[2560,3456]{1,0:T(8,128)(2,1)} copy(bf16[2560,3456]{1,0:T(8,128)(2,1)} %all-gather.8.cloned.1.call-done) | data formatting | bytes 35389440
Async XLA Ops:
  7.2 174.9 %all-gather.4.cloned.1.call-start = ((), (), s32[]{:S(2)}) async-start(), calls=%async_computation.2 | async-start | bytes 21233664 | tf_op jit(solution)/shard_map/all_gather | solution.py:14
  7.9 359.6 %all-gather.6.cloned.1.call-start = ((), (), s32[]{:S(2)}) async-start(), calls=%async_computation.4 | async-start | bytes 13107200 | tf_op jit(solution)/shard_map/all_gather | solution.py:12
  8.6 533.5 %reduce-scatter.5.cloned.1.call-start = ((), (), s32[]{:S(2)}) async-start(), calls=%async_computation.5 | async-start | bytes 22118400 | tf_op jit(solution)/shard_map/reduce_scatter | solution.py:25
  413.2 478.6 %reduce-scatter.3.cloned.1.call-start = ((), (), s32[]{:S(2)}) async-start(), calls=%async_computation.3 | async-start | bytes 26214400 | tf_op jit(solution)/shard_map/reduce_scatter | solution.py:16
  460.5 548.0 %all-gather.8.cloned.1.call-start = ((), (), s32[]{:S(2)}) async-start(), calls=%async_computation.6 | async-start | bytes 22118400 | tf_op jit(solution)/shard_map/all_gather | solution.py:41
Sparse Core Ops, SparseCore 0:
  9.5 172.4 all-gather.3
  183.6 183.8 all-gather.5
  413.3 128.7 reduce-scatter.4
  544.3 347.3 reduce-scatter.2
  893.7 114.7 all-gather.7
where the time goes:
time: 1030 us
  waiting for transfers between devices  881 us (86%)
  matrix products  92.9 us (9%)
  other arithmetic  27.3 us (3%)
  local copies, waits for them, and re-layouts  16 us (2%)
  between operations  13.8 us (1%)
    reduce_scatter x1, waiting for transfers between devices, per_device(): lax.psum_scatter(lax.dot_general(picked, weight, (((1,), (1,)), ((), ()))...  327 us
    all_gather x1, waiting for transfers between devices, per_device(): whole_acts = lax.all_gather(acts, 'col', axis=0, tiled=True)  185 us
    all_gather x1, waiting for transfers between devices, per_device(): whole_cotangent = lax.all_gather(grad_out, 'row', axis=0, tiled=True)  173 us
    all_gather x1, waiting for transfers between devices, per_device(): lax.all_gather(new_master.astype(jnp.bfloat16), 'depth', axis=0, tiled=True)  113 us
    reduce_scatter x1, waiting for transfers between devices, per_device(): lax.psum_scatter(lax.dot_general(picked, whole_cotangent, (((0,), (0,)),...  81.3 us
    dot_general x1, matrix products, per_device(): lax.dot_general(picked, weight, (((1,), (1,)), ((), ())), preferred_eleme...  47.3 us
    dot_general x1, matrix products, per_device(): lax.dot_general(picked, whole_cotangent, (((0,), (0,)), ((), ())), prefer...  45.6 us
    convert_element_type x1, other arithmetic, per_device(): new_master.astype(jnp.bfloat16)  23 us
  transfers between devices with their start and end apart: 5, of which 5 were waited for; matrix products, arithmetic and copies ran while one was open for 7% of the time, Pallas kernels for 0%

commit v1 on v0

v1 whole, which is shorter than its diff:
```python
import functools
import math

import jax
import jax.numpy as jnp
from jax import lax
from jax.experimental import pallas as pl
from jax.sharding import PartitionSpec as P


STEP = 10
LANES = 128


def adamw(grad, master, moment_one, moment_two):
    new_moment_one = 0.9 * moment_one + 0.1 * grad
    new_moment_two = 0.95 * moment_two + 0.05 * grad * grad
    first_fix = 1.0 - 0.9**STEP
    second_fix = 1.0 - 0.95**STEP
    update = new_moment_one / first_fix / (jnp.sqrt(new_moment_two / second_fix) + 1e-08)
    new_master = master - 0.01 * (update + 0.1 * master)
    return new_master, new_moment_one, new_moment_two


def general(acts, grad_out, weight, master, moment_one, moment_two):
    whole_acts = lax.all_gather(acts, "col", axis=0, tiled=True)
    tokens_total = acts.shape[0] * lax.axis_size("col") * lax.axis_size("depth")
    whole_cotangent = lax.all_gather(grad_out, "row", axis=0, tiled=True)
    input_sum = lax.psum_scatter(
        lax.dot_general(
            whole_cotangent, weight, (((1,), (1,)), ((), ())), preferred_element_type=jnp.float32
        ),
        "col",
        scatter_dimension=0,
        tiled=True,
    )
    grad_sum = lax.psum_scatter(
        lax.dot_general(
            whole_acts, whole_cotangent, (((0,), (0,)), ((), ())), preferred_element_type=jnp.float32
        ).astype(jnp.bfloat16),
        "depth",
        scatter_dimension=0,
        tiled=True,
    ).astype(jnp.float32)
    grad = grad_sum * jnp.float32(1.0 / math.sqrt(tokens_total))
    updated = adamw(grad, master, moment_one, moment_two)
    new_weight = lax.all_gather(updated[0].astype(jnp.bfloat16), "depth", axis=0, tiled=True)
    return (input_sum.astype(jnp.bfloat16), new_weight) + updated


def update_kernel(scale, mine, near, far, master, one, two, *rest):
    out_master, out_one, out_two, out_weight = rest[-4:]
    f32 = jnp.float32
    grad = (mine[...].astype(f32) + near[...].astype(f32) + far[...].astype(f32)) * scale
    new_master, new_one, new_two = adamw(grad, master[...], one[...], two[...])
    out_master[...] = new_master
    out_one[...] = new_one
    out_two[...] = new_two
    out_weight[...] = new_master.astype(out_weight.dtype)


def update_chunk(scale, start, width, mine, near, far, state, previous):
    rows = mine.shape[0]
    block = LANES * math.gcd(start // LANES, width // LANES) if start else width
    while rows * block > 2**18 and block % (2 * LANES) == 0:
        block //= 2
    if rows * block > 2**18:
        block = LANES
    offset = start // block
    part = pl.BlockSpec((rows, block), lambda i: (0, i))
    placed = pl.BlockSpec((rows, block), lambda i: (0, i + offset))
    whole = jax.ShapeDtypeStruct(state[0].shape, state[0].dtype)
    return pl.pallas_call(
        functools.partial(update_kernel, scale),
        grid=(width // block,),
        in_specs=[part] * 3 + [placed] * 3 + [pl.BlockSpec(memory_space=pl.ANY)] * len(previous),
        out_specs=[placed] * 3 + [part],
        out_shape=[whole] * 3 + [jax.ShapeDtypeStruct((rows, width), jnp.bfloat16)],
        input_output_aliases={6 + i: i for i in range(len(previous))},
        cost_estimate=pl.CostEstimate(
            flops=20 * rows * width, bytes_accessed=32 * rows * width, transcendentals=rows * width
        ),
    )(mine, near, far, *state, *previous)


def cuts(columns, weights=(9, 9, 9)):
    units = columns // LANES
    total, at, result = sum(weights), 0, []
    run = 0
    for w in weights:
        run += w
        end = units * run // total
        result.append((at * LANES, (end - at) * LANES))
        at = end
    return result


def tie(value, *after):
    return lax.optimization_barrier((value,) + after)[0]


def per_device(*operands):
    return step(*operands)


def step(acts, grad_out, weight, master, moment_one, moment_two):
    f32, bf16 = jnp.float32, jnp.bfloat16
    cols, depths = lax.axis_size("col"), lax.axis_size("depth")
    row, col, depth = (lax.axis_index(a) for a in ("row", "col", "depth"))
    side, core = depth // 2, depth % 2
    tokens, width = acts.shape
    half, shard = width // 2, width // depths
    columns = grad_out.shape[1]
    scale = 1.0 / math.sqrt(tokens * cols * depths)
    swap_row = [(0, 1), (1, 0)]
    swap_side = [(0, 2), (2, 0), (1, 3), (3, 1)]
    swap_core = [(0, 1), (1, 0), (2, 3), (3, 2)]
    pieces = cuts(columns)

    far_cot = [
        lax.ppermute(lax.slice_in_dim(grad_out, s, s + w, axis=1), "row", swap_row)
        for s, w in pieces
    ]

    def input_rows(q):
        return lax.slice_in_dim(weight, q * half, (q + 1) * half, axis=0)

    def dot_in(cot, w):
        return lax.dot_general(cot, w, (((1,), (1,)), ((), ())), preferred_element_type=f32)

    heres = [dot_in(grad_out, input_rows(q)) for q in range(2)]

    def add_there(total, i, far):
        s, w = pieces[i]
        terms = [dot_in(far, lax.slice_in_dim(input_rows(q), s, s + w, axis=1)) for q in range(2)]
        return terms if total is None else [a + b for a, b in zip(total, terms)]

    there = add_there(None, 0, far_cot[0])

    def gather_line(block, after):
        rights, lefts = [block], [block]
        for s in range(1, cols):
            if s in after:
                rights[-1] = tie(rights[-1], *after[s])
                lefts[-1] = tie(lefts[-1], *after[s])
            rights.append(
                lax.ppermute(rights[-1], "col", [(i, i + 1) for i in range(s - 1, cols - 1)])
            )
            lefts.append(
                lax.ppermute(lefts[-1], "col", [(i, i - 1) for i in range(1, cols - s + 1)])
            )
        return rights, lefts

    def assemble(rights, lefts, *after):
        block = rights[0]
        rights = [tie(v, *after) for v in rights]
        lefts = [tie(v, *after) for v in lefts]
        out = jnp.zeros((cols * tokens, block.shape[1]), block.dtype)
        out = lax.dynamic_update_slice(out, block, (col * tokens, 0))
        for s in range(1, cols):
            picked = jnp.where(col >= s, rights[s], lefts[cols - s])
            at = lax.rem(col - s + cols, cols) * tokens
            out = lax.dynamic_update_slice(out, picked, (at, 0))
        return out

    def acts_of(which):
        return lax.dynamic_slice_in_dim(acts, which * half, half, axis=1)

    rights, lefts = gather_line(acts_of(1 - side), {2: (heres[0],), 3: (heres[1], *there)})
    acts_away = assemble(rights, lefts, heres[0])
    third_away = (rights[3], lefts[3])
    rights, lefts = gather_line(tie(acts_of(side), rights[2], lefts[2]), {})
    early_after = (rights[1], lefts[1])

    def grad_part(whole_acts, cot):
        out = lax.dot_general(
            whole_acts, cot, (((0,), (0,)), ((), ())), preferred_element_type=f32
        ).astype(bf16)
        mine = lax.dynamic_slice_in_dim(out, core * shard, shard, axis=0)
        give = lax.dynamic_slice_in_dim(out, (1 - core) * shard, shard, axis=0)
        return mine, lax.ppermute(give, "depth", swap_core)

    later_cot = tie(grad_out, heres[0])

    cots, sums = [], []
    for i, ((s, w), far) in enumerate(zip(pieces, far_cot)):
        if i == 0:
            far = tie(far, *there)
        if i == 1:
            far = tie(far, mine, *third_away)
        if i == 2:
            far = tie(far, mine, *there)
        near = lax.slice_in_dim(later_cot, s, s + w, axis=1)
        cot = jnp.zeros((2 * near.shape[0], w), near.dtype)
        cot = lax.dynamic_update_slice(cot, near, (row * near.shape[0], 0))
        cot = lax.dynamic_update_slice(cot, far, ((1 - row) * near.shape[0], 0))
        cots.append(cot)
        mine, near = grad_part(acts_away, cot)
        both = (mine.astype(f32) + near.astype(f32)).astype(bf16)
        sums.append(lax.ppermute(both, "depth", swap_side))
        if i > 0:
            there = add_there(there, i, tie(far, both))

    acts_home = assemble(rights, lefts, *there)

    state, previous = (master, moment_one, moment_two), ()
    new_weight = jnp.zeros(weight.shape, bf16)
    for (s, w), cot, far in zip(pieces, cots, sums):
        mine, near = grad_part(acts_home, cot)
        *previous, fresh = update_chunk(scale, s, w, mine, near, far, state, tuple(previous))
        across = lax.ppermute(fresh, "depth", swap_side)
        beside = lax.ppermute(fresh, "depth", swap_core)
        diagonal = lax.ppermute(across, "depth", swap_core)
        for block, a, b in (
            (fresh, side, core),
            (beside, side, 1 - core),
            (across, 1 - side, core),
            (diagonal, 1 - side, 1 - core),
        ):
            new_weight = lax.dynamic_update_slice(new_weight, block, ((2 * a + b) * shard, s))

    place = jnp.where(row == 0, col, cols - 1 - col)

    def hop(value, pairs):
        where = lambda r, m: r * cols + (m if r == 0 else cols - 1 - m)
        return lax.ppermute(
            value, ("row", "col"), [(where(r, a), where(r, b)) for r in (0, 1) for a, b in pairs]
        )

    def chain(first, second, at, flip):
        go = lambda v, pairs: hop(v, [(cols - 1 - a, cols - 1 - b) for a, b in pairs] if flip else pairs)
        got = go(first.astype(bf16), [(3, 2)])
        beside = go(second.astype(bf16), [(0, 1)])
        out = jnp.where(at == 3, second, first + got.astype(f32)).astype(bf16)
        got = go(out, [(3, 2), (2, 1)])
        out = (jnp.where(at == 1, first, second) + got.astype(f32)).astype(bf16)
        got = go(out, [(2, 1), (1, 0)])
        return beside.astype(f32) + got.astype(f32)

    def picked(block, first):
        return lax.dynamic_slice_in_dim(block, first * tokens, tokens, axis=0)

    outs = []
    for q in range(2):
        here = heres[q]
        p0, p1 = picked(here, row), picked(here, 1 - row)
        p2, p3 = picked(there[q], row), picked(there[q], 1 - row)
        q0, q1 = lax.optimization_barrier((p0, p1) + early_after)[:2]
        early = chain(q0, q1, place, False)
        late = chain(p3, p2, cols - 1 - place, True)
        own = jnp.where(place < 2, jnp.where(place == 0, p0, p1), jnp.where(place == 2, p2, p3))
        outs.append((own + jnp.where(place < 2, early, late)).astype(bf16))
    grad_in = jnp.concatenate(outs, axis=1)
    return (grad_in, new_weight) + tuple(previous)


def solution(mesh):
    shape = mesh.shape
    fits = shape["row"] == 2 and shape["col"] == 4 and shape["depth"] == 4
    state = P(("row", "depth"), "col")
    return jax.shard_map(
        per_device if fits else general,
        mesh=mesh,
        in_specs=(P(("depth", "col"), "row"), P(("depth", "row"), "col"), P("row", "col")) + (state,) * 3,
        out_specs=(P(("depth", "col"), "row"), P("row", "col")) + (state,) * 3,
        check_vma=False,
    )
```

time: 1030 us -> 670 us (0.65); the launches traced: 1030 us -> 660 us
  waiting for transfers between devices: 881 us -> 239 us
  starting transfers between devices: 0.38 us -> 118 us
  local copies, waits for them, and re-layouts: 16 us -> 78.6 us
  matrix products: 92.9 us -> 137 us
  Pallas kernels: 0 us -> 38.8 us
  other arithmetic: 27.3 us -> 46.4 us
  between operations: 13.8 us -> 1.91 us
    all_gather x3 -> x0, waiting for transfers between devices: 471 us -> none  [the longest x1 185 us: per_device(): whole_acts = lax.all_gather(acts, 'col', axis=0, tiled=True)]
    reduce_scatter x2 -> x0, waiting for transfers between devices: 408 us -> none  [the longest x1 327 us: per_device(): lax.psum_scatter(lax.dot_general(picked, weight, (((1,), (1,)), ((), ()))...]
    ppermute x0 -> x49, waiting for transfers between devices: none -> 239 us  [the longest x3 117 us: step(): lax.ppermute(lax.slice_in_dim(grad_out, s, s + w, axis=1), 'row', swap_row)]
    ppermute x0 -> x49, starting transfers between devices: none -> 118 us  [the longest x16 81.8 us: hop(): lax.ppermute(value, ('row', 'col'), [(where(r, a), where(r, b)) for r in...]
    dynamic_update_slice x0 -> x20, local copies, waits for them, and re-layouts: none -> 44.6 us  [the longest x12 25.7 us: step(): lax.dynamic_update_slice(new_weight, block, ((2 * a + b) * shard, s))]
    dot_general x2 -> x14, matrix products: 92.9 us -> 137 us  [the longest x8 82.2 us: dot_in(): lax.dot_general(cot, w, (((1,), (1,)), ((), ())), preferred_element_type=...]
    pallas_call x0 -> x3, Pallas kernels: none -> 38.8 us  [update_chunk(): pl.pallas_call(functools.partial(update_kernel, scale), grid=(width // bl...]
    unnamed x1 -> x58, local copies, waits for them, and re-layouts: 16 us -> 3.79 us
  transfers between devices with their start and end apart: 5 -> 49, of which waited for: 5 -> 7; matrix products, arithmetic and copies ran while one was open for 7% -> 38% of each run, Pallas kernels for 0% -> 6%
where the time goes in v1:
time: 670 us; the launch traced here: 660 us
  waiting for transfers between devices  239 us (36%)
  matrix products  137 us (20%)
  starting transfers between devices  118 us (18%)
  local copies, waits for them, and re-layouts  78.6 us (12%)
  other arithmetic  46.4 us (7%)
  Pallas kernels  38.8 us (6%)
    ppermute x3, waiting for transfers between devices, step(): lax.ppermute(lax.slice_in_dim(grad_out, s, s + w, axis=1), 'row', swap_row)  117 us
    dot_general x8, matrix products, dot_in(): lax.dot_general(cot, w, (((1,), (1,)), ((), ())), preferred_element_type=...  82.2 us
    ppermute x16, starting transfers between devices, hop(): lax.ppermute(value, ('row', 'col'), [(where(r, a), where(r, b)) for r in...  81.8 us
    dot_general x6, matrix products, grad_part(): lax.dot_general(whole_acts, cot, (((0,), (0,)), ((), ())), preferred_elem...  54.8 us
    ppermute x3, waiting for transfers between devices, step(): across = lax.ppermute(fresh, 'depth', swap_side)  46.5 us
    ppermute x16, waiting for transfers between devices, hop(): lax.ppermute(value, ('row', 'col'), [(where(r, a), where(r, b)) for r in...  43.7 us
    pallas_call x3, Pallas kernels, update_chunk(): pl.pallas_call(functools.partial(update_kernel, scale), grid=(width // bl...  38.8 us
    ppermute x6, waiting for transfers between devices, gather_line(): lax.ppermute(lefts[-1], 'col', [(i, i - 1) for i in range(1, cols - s + 1)])  31.9 us
  transfers between devices with their start and end apart: 49, of which 7 were waited for; matrix products, arithmetic and copies ran while one was open for 38% of the time, Pallas kernels for 6%

profile of v1, /device:TPU:0, one launch (start us, length us, event | category | flops | bytes accessed | tf_op | source)
XLA Modules:
  0.0 660.2 jit_solution(12455277692252144413)
XLA Ops:
  7.9 6.1 collective-permute-start.2
  21.9 14.9 %fusion.2 = f32[1024,1280]{1,0:T(8,128)} fusion(bf16[1024,3456]{1,0:T(8,128)(2,1)S(1)} %copy-done.2, bf16[2560,3456]{1,0:T(8,128)(2,1)} %param.8), kind=kOutput, calls=%fused_computation.2 | convolution fusion | flops 9059696640 | bytes 21168128 | tf_op jit(solution)/shard_map/dot_general | solution.py:129
  36.8 15.9 %fusion = f32[1024,1280]{1,0:T(8,128)} fusion(bf16[1024,3456]{1,0:T(8,128)(2,1)} %param.7, bf16[2560,3456]{1,0:T(8,128)(2,1)} %param.8), kind=kOutput, calls=%fused_computation | convolution fusion | flops 9059696640 | bytes 21168128 | tf_op jit(solution)/shard_map/dot_general | solution.py:129
  55.7 116.8 %collective-permute-done = bf16[1024,1152]{1,0:T(8,128)(2,1)} collective-permute-done((bf16[1024,1152]{1,0:T(8,128)(2,1)}, bf16[1024,1152]{1,0:T(8,128)(2,1)}, u32[]{:S(2)}, u32[]{:S(2)}) %collective-permute-start) | collective-permute-done | bytes 2359328 | tf_op jit(solution)/shard_map/ppermute | solution.py:121
  172.5 8.5 %fusion.8 = f32[1024,1280]{1,0:T(8,128)} fusion(bf16[1024,1152]{1,0:T(8,128)(2,1)} %collective-permute-done, bf16[2560,3456]{1,0:T(8,128)(2,1)} %param.8), kind=kOutput, calls=%fused_computation.21 | convolution fusion | flops 3019898880 | bytes 10551296 | tf_op jit(solution)/shard_map/dot_general | solution.py:129
  181.0 8.5 %fusion.10 = f32[1024,1280]{1,0:T(8,128)} fusion(bf16[1024,1152]{1,0:T(8,128)(2,1)} %collective-permute-done, bf16[2560,3456]{1,0:T(8,128)(2,1)} %param.8), kind=kOutput, calls=%fused_computation.23 | convolution fusion | flops 3019898880 | bytes 10551296 | tf_op jit(solution)/shard_map/dot_general | solution.py:129
  204.2 19.2 %collective-permute-done.5 = bf16[512,1280]{1,0:T(8,128)(2,1)} collective-permute-done((bf16[512,1280]{1,0:T(8,128)(2,1)}, bf16[512,1280]{1,0:T(8,128)(2,1)}, u32[]{:S(2)}, u32[]{:S(2)}) %collective-permute-start.5) | collective-permute-done | bytes 1310752 | tf_op jit(solution)/shard_map/ppermute | solution.py:150
  232.6 9.0 %convolution_convert_fusion.5 = bf16[1280,1152]{1,0:T(8,128)(2,1)S(1)} fusion(bf16[2048,1280]{1,0:T(8,128)(2,1)} %select_dynamic-update-slice_fusion.3, bf16[2048,1152]{1,0:T(8,128)(2,1)S(1)} %constant_dynamic-update-slice_fusion.7), kind=kOutput, calls=%fused_computation.9 | convolution fusion | flops 6041272320 | bytes 12910592 | tf_op jit(solution)/shard_map/dot_general | solution.py:176
  243.2 4.9 constant_dynamic-slice_fusion.7
  260.3 10.8 %convolution_convert_fusion.4 = bf16[1280,1152]{1,0:T(8,128)(2,1)S(1)} fusion(bf16[2048,1280]{1,0:T(8,128)(2,1)} %select_dynamic-update-slice_fusion.3, bf16[2048,1152]{1,0:T(8,128)(2,1)S(1)} %constant_dynamic-update-slice_fusion.6), kind=kOutput, calls=%fused_computation.8 | convolution fusion | flops 6041272320 | bytes 12910592 | tf_op jit(solution)/shard_map/dot_general | solution.py:176
  273.6 12.8 %collective-permute-done.29 = bf16[512,1280]{1,0:T(8,128)(2,1)} collective-permute-done((bf16[512,1280]{1,0:T(8,128)(2,1)}, bf16[512,1280]{1,0:T(8,128)(2,1)}, u32[]{:S(2)}, u32[]{:S(2)}) %collective-permute-start.29) | collective-permute-done | bytes 1310752 | tf_op jit(solution)/shard_map/ppermute | solution.py:150
  291.7 10.0 %convolution_add_fusion.2 = f32[1024,1280]{1,0:T(8,128)} fusion(f32[1024,1280]{1,0:T(8,128)} %fusion.8, bf16[1024,1152]{1,0:T(8,128)(2,1)} %collective-permute-done.1, bf16[2560,3456]{1,0:T(8,128)(2,1)} %param.8), kind=kOutput, calls=%fused_computation.12 | convolution fusion | flops 3021209600 | bytes 15794176 | tf_op jit(solution)/shard_map/dot_general | solution.py:129
  301.7 10.0 %convolution_add_fusion.3 = f32[1024,1280]{1,0:T(8,128)} fusion(f32[1024,1280]{1,0:T(8,128)} %fusion.10, bf16[1024,1152]{1,0:T(8,128)(2,1)} %collective-permute-done.1, bf16[2560,3456]{1,0:T(8,128)(2,1)} %param.8), kind=kOutput, calls=%fused_computation.13 | convolution fusion | flops 3021209600 | bytes 15794176 | tf_op jit(solution)/shard_map/dot_general | solution.py:129
  316.5 10.4 %convolution_convert_fusion.3 = bf16[1280,1152]{1,0:T(8,128)(2,1)S(1)} fusion(bf16[2048,1280]{1,0:T(8,128)(2,1)} %select_dynamic-update-slice_fusion.3, bf16[2048,1152]{1,0:T(8,128)(2,1)} %constant_dynamic-update-slice_fusion.5), kind=kOutput, calls=%fused_computation.7 | convolution fusion | flops 6041272320 | bytes 12910592 | tf_op jit(solution)/shard_map/dot_general | solution.py:176
  329.2 47.3 %collective-permute-start.21 = (bf16[512,1280]{1,0:T(8,128)(2,1)}, bf16[512,1280]{1,0:T(8,128)(2,1)S(1)}, u32[]{:S(2)}, u32[]{:S(2)}) collective-permute-start(bf16[512,1280]{1,0:T(8,128)(2,1)} %get-tuple-element.108), channel_id=1, source_target_pairs={{0,4},{28,24},{1,5},{29,25},{2,6},{30,26},{3,7},{31,27}} | collective-permute-start | bytes 3932168 | tf_op jit(solution)/shard_map/ppermute | solution.py:226
  380.2 6.3 convolution_add_fusion
  386.5 8.1 %convolution_add_fusion.1 = f32[1024,1280]{1,0:T(8,128)S(1)} fusion(f32[1024,1280]{1,0:T(8,128)S(1)} %bitcast.33, bf16[1024,1152]{1,0:T(8,128)(2,1)} %collective-permute-done.9, bf16[2560,3456]{1,0:T(8,128)(2,1)} %param.8), kind=kOutput, calls=%fused_computation.11 | convolution fusion | flops 3021209600 | bytes 15794176 | tf_op jit(solution)/shard_map/dot_general | solution.py:129
  394.6 4.6 collective-permute-start.13
  406.2 9.8 %convolution_convert_fusion = bf16[1280,1152]{1,0:T(8,128)(2,1)S(1)} fusion(bf16[2048,1280]{1,0:T(8,128)(2,1)S(1)} %select_dynamic-update-slice_fusion, bf16[2048,1152]{1,0:T(8,128)(2,1)} %constant_dynamic-update-slice_fusion.5), kind=kOutput, calls=%fused_computation.4 | convolution fusion | flops 6041272320 | bytes 12910592 | tf_op jit(solution)/shard_map/dot_general | solution.py:176
  416.0 7.4 %convolution_convert_fusion.1 = bf16[1280,1152]{1,0:T(8,128)(2,1)S(1)} fusion(bf16[2048,1280]{1,0:T(8,128)(2,1)S(1)} %select_dynamic-update-slice_fusion, bf16[2048,1152]{1,0:T(8,128)(2,1)S(1)} %bitcast.29), kind=kOutput, calls=%fused_computation.5 | convolution fusion | flops 6041272320 | bytes 12910592 | tf_op jit(solution)/shard_map/dot_general | solution.py:176
  437.9 7.4 %convolution_convert_fusion.2 = bf16[1280,1152]{1,0:T(8,128)(2,1)S(1)} fusion(bf16[2048,1280]{1,0:T(8,128)(2,1)S(1)} %select_dynamic-update-slice_fusion, bf16[2048,1152]{1,0:T(8,128)(2,1)S(1)} %bitcast.31), kind=kOutput, calls=%fused_computation.6 | convolution fusion | flops 6041272320 | bytes 12910592 | tf_op jit(solution)/shard_map/dot_general | solution.py:176
  448.3 41.0 %collective-permute-done.26 = bf16[512,1280]{1,0:T(8,128)(2,1)} collective-permute-done((bf16[512,1280]{1,0:T(8,128)(2,1)}, bf16[512,1280]{1,0:T(8,128)(2,1)}, u32[]{:S(2)}, u32[]{:S(2)}) %collective-permute-start.26) | collective-permute-done | bytes 1310752 | tf_op jit(solution)/shard_map/ppermute | solution.py:226
  490.0 4.4 select_convert_fusion
  494.5 5.4 collective-permute-start.27
  505.8 5.6 collective-permute-start.19
  511.4 12.9 %shard_map.101 = (f32[640,3456]{1,0:T(8,128)}, f32[640,3456]{1,0:T(8,128)}, f32[640,3456]{1,0:T(8,128)}, bf16[640,1152]{1,0:T(8,128)(2,1)}) custom-call(bf16[640,1152]{1,0:T(8,128)(2,1)} %get-tuple-element.105.mine, bf16[640,1152]{1,0:T(8,128)(2,1)} %collective-permute-done.33.near, bf16[640,1152]{1,0:T(8,128)(2,1)} %collective-permute-done.35.far, ...), custom_call_target="tpu_custom_call" | custom-call | flops 14745600 | bytes 23592960 | tf_op jit(solution)/shard_map/pallas_call | solution.py:73
  528.3 12.9 %shard_map.102 = (f32[640,3456]{1,0:T(8,128)}, f32[640,3456]{1,0:T(8,128)}, f32[640,3456]{1,0:T(8,128)}, bf16[640,1152]{1,0:T(8,128)(2,1)}) custom-call(bf16[640,1152]{1,0:T(8,128)(2,1)} %get-tuple-element.103.mine, bf16[640,1152]{1,0:T(8,128)(2,1)} %collective-permute-done.39.near, ...), custom_call_target="tpu_custom_call", output_to_operand_aliasing={{0}: (6, {}), {1}: (7, {}), {2}: (8, {})} | custom-call | flops 14745600 | bytes 23592960 | tf_op jit(solution)/shard_map/pallas_call | solution.py:73
  541.3 12.9 %shard_map.103 = (f32[640,3456]{1,0:T(8,128)}, f32[640,3456]{1,0:T(8,128)}, f32[640,3456]{1,0:T(8,128)}, bf16[640,1152]{1,0:T(8,128)(2,1)}) custom-call(bf16[640,1152]{1,0:T(8,128)(2,1)} %get-tuple-element.101.mine, bf16[640,1152]{1,0:T(8,128)(2,1)} %collective-permute-done.44.near, ...), custom_call_target="tpu_custom_call", output_to_operand_aliasing={{0}: (6, {}), {1}: (7, {}), {2}: (8, {})} | custom-call | flops 14745600 | bytes 23592960 | tf_op jit(solution)/shard_map/pallas_call | solution.py:73
  558.7 6.3 broadcast_in_dim.3
  580.1 5.8 add_convert_fusion.3
  586.3 15.4 %collective-permute-done.47 = bf16[640,1152]{1,0:T(8,128)(2,1)} collective-permute-done((bf16[640,1152]{1,0:T(8,128)(2,1)}, bf16[640,1152]{1,0:T(8,128)(2,1)}, u32[]{:S(2)}, u32[]{:S(2)}) %collective-permute-start.47) | collective-permute-done | bytes 1474592 | tf_op jit(solution)/shard_map/ppermute | solution.py:211
  601.7 31.1 %collective-permute-done.42 = bf16[640,1152]{1,0:T(8,128)(2,1)} collective-permute-done((bf16[640,1152]{1,0:T(8,128)(2,1)}, bf16[640,1152]{1,0:T(8,128)(2,1)}, u32[]{:S(2)}, u32[]{:S(2)}) %collective-permute-start.42) | collective-permute-done | bytes 1474592 | tf_op jit(solution)/shard_map/ppermute | solution.py:211
  (207 shorter events, 155.7 us)
Async XLA Ops:
  7.9 44.8 %collective-permute-start.2 = (bf16[512,1280]{1,0:T(8,128)(2,1)}, bf16[512,1280]{1,0:T(8,128)(2,1)}, u32[]{:S(2)}, u32[]{:S(2)}) collective-permute-start(bf16[512,1280]{1,0:T(8,128)(2,1)} %get-tuple-element.88), channel_id=1, source_target_pairs={{0,4},{4,8},{8,12},{1,5},{5,9},{9,13},{2,6},{6,10},{10,14},{3,7},{... | collective-permute-start | bytes 3932168 | tf_op jit(solution)/shard_map/ppermute | solution.py:147
  14.0 40.5 %collective-permute-start.3 = (bf16[512,1280]{1,0:T(8,128)(2,1)}, bf16[512,1280]{1,0:T(8,128)(2,1)S(1)}, u32[]{:S(2)}, u32[]{:S(2)}) collective-permute-start(bf16[512,1280]{1,0:T(8,128)(2,1)} %get-tuple-element.88), channel_id=1, source_target_pairs={{4,0},{8,4},{12,8},{5,1},{9,5},{13,9},{6,2},{10,6},{14,10},{7,3},{... | collective-permute-start | bytes 3932168 | tf_op jit(solution)/shard_map/ppermute | solution.py:150
  18.4 293.4 %collective-permute-start.9 = (bf16[1024,1152]{1,0:T(8,128)(2,1)}, bf16[1024,1152]{1,0:T(8,128)(2,1)}, u32[]{:S(2)}, u32[]{:S(2)}) collective-permute-start(bf16[1024,1152]{1,0:T(8,128)(2,1)} %get-tuple-element.89), channel_id=1, source_target_pairs={{0,16},{16,0},{1,17},{17,1},{2,18},{18,2},{3,19},{19,3},{4,20},{20... | collective-permute-start | bytes 7077896 | tf_op jit(solution)/shard_map/ppermute | solution.py:121
  19.9 236.2 %collective-permute-start.1 = (bf16[1024,1152]{1,0:T(8,128)(2,1)}, bf16[1024,1152]{1,0:T(8,128)(2,1)}, u32[]{:S(2)}, u32[]{:S(2)}) collective-permute-start(bf16[1024,1152]{1,0:T(8,128)(2,1)} %get-tuple-element.90), channel_id=1, source_target_pairs={{0,16},{16,0},{1,17},{17,1},{2,18},{18,2},{3,19},{19,3},{4,20},{20... | collective-permute-start | bytes 7077896 | tf_op jit(solution)/shard_map/ppermute | solution.py:121
  20.4 152.1 %collective-permute-start = (bf16[1024,1152]{1,0:T(8,128)(2,1)}, bf16[1024,1152]{1,0:T(8,128)(2,1)}, u32[]{:S(2)}, u32[]{:S(2)}) collective-permute-start(bf16[1024,1152]{1,0:T(8,128)(2,1)} %get-tuple-element.91), channel_id=1, source_target_pairs={{0,16},{16,0},{1,17},{17,1},{2,18},{18,2},{3,19},{19,3},{4,20},{20... | collective-permute-start | bytes 7077896 | tf_op jit(solution)/shard_map/ppermute | solution.py:121
  52.7 136.8 %collective-permute-start.6 = (bf16[512,1280]{1,0:T(8,128)(2,1)}, bf16[512,1280]{1,0:T(8,128)(2,1)}, u32[]{:S(2)}, u32[]{:S(2)}) collective-permute-start(bf16[512,1280]{1,0:T(8,128)(2,1)} %collective-permute-done.2), channel_id=1, source_target_pairs={{4,8},{8,12},{5,9},{9,13},{6,10},{10,14},{7,11},{11,15},{20,24},{2... | collective-permute-start | bytes 3932168 | tf_op jit(solution)/shard_map/ppermute | solution.py:147
  54.5 135.1 %collective-permute-start.4 = (bf16[512,1280]{1,0:T(8,128)(2,1)S(1)}, bf16[512,1280]{1,0:T(8,128)(2,1)}, u32[]{:S(2)}, u32[]{:S(2)}) collective-permute-start(bf16[512,1280]{1,0:T(8,128)(2,1)S(1)} %collective-permute-done.3), channel_id=1, source_target_pairs={{4,0},{8,4},{5,1},{9,5},{6,2},{10,6},{7,3},{11,7},{20,16},{24,20},... | collective-permute-start | bytes 3932168 | tf_op jit(solution)/shard_map/ppermute | solution.py:150
  202.9 48.1 %collective-permute-start.12 = (bf16[512,1280]{1,0:T(8,128)(2,1)S(1)}, bf16[512,1280]{1,0:T(8,128)(2,1)}, u32[]{:S(2)}, u32[]{:S(2)}) collective-permute-start(bf16[512,1280]{1,0:T(8,128)(2,1)S(1)} %get-tuple-element.60), channel_id=1, source_target_pairs={{4,0},{8,4},{12,8},{5,1},{9,5},{13,9},{6,2},{10,6},{14,10},{7,3},{... | collective-permute-start | bytes 3932168 | tf_op jit(solution)/shard_map/ppermute | solution.py:150
  272.4 54.7 %collective-permute-start.23 = (bf16[512,1280]{1,0:T(8,128)(2,1)S(1)}, bf16[512,1280]{1,0:T(8,128)(2,1)S(1)}, u32[]{:S(2)}, u32[]{:S(2)}) collective-permute-start(bf16[512,1280]{1,0:T(8,128)(2,1)S(1)} %select_convert_fusion.1), channel_id=1, source_target_pairs={{12,8},{8,4},{16,20},{20,24},{13,9},{9,5},{17,21},{21,25},{14,10},... | collective-permute-start | bytes 3932168 | tf_op jit(solution)/shard_map/ppermute | solution.py:226
  286.4 42.8 %collective-permute-start.15 = (bf16[512,1280]{1,0:T(8,128)(2,1)S(1)}, bf16[512,1280]{1,0:T(8,128)(2,1)S(1)}, u32[]{:S(2)}, u32[]{:S(2)}) collective-permute-start(bf16[512,1280]{1,0:T(8,128)(2,1)S(1)} %select_convert_fusion.3), channel_id=1, source_target_pairs={{12,8},{8,4},{16,20},{20,24},{13,9},{9,5},{17,21},{21,25},{14,10},... | collective-permute-start | bytes 3932168 | tf_op jit(solution)/shard_map/ppermute | solution.py:226
  287.1 112.1 %collective-permute-start.30 = (bf16[512,1280]{1,0:T(8,128)(2,1)}, bf16[512,1280]{1,0:T(8,128)(2,1)}, u32[]{:S(2)}, u32[]{:S(2)}) collective-permute-start(bf16[512,1280]{1,0:T(8,128)(2,1)} %collective-permute-done.29), channel_id=1, source_target_pairs={{4,0},{5,1},{6,2},{7,3},{20,16},{21,17},{22,18},{23,19}} | collective-permute-start | bytes 3932168 | tf_op jit(solution)/shard_map/ppermute | solution.py:150
  288.4 106.2 %collective-permute-start.32 = (bf16[512,1280]{1,0:T(8,128)(2,1)}, bf16[512,1280]{1,0:T(8,128)(2,1)}, u32[]{:S(2)}, u32[]{:S(2)}) collective-permute-start(bf16[512,1280]{1,0:T(8,128)(2,1)} %collective-permute-done.31), channel_id=1, source_target_pairs={{8,12},{9,13},{10,14},{11,15},{24,28},{25,29},{26,30},{27,31}} | collective-permute-start | bytes 3932168 | tf_op jit(solution)/shard_map/ppermute | solution.py:147
  311.8 118.8 %collective-permute-start.35 = (bf16[640,1152]{1,0:T(8,128)(2,1)S(1)}, bf16[640,1152]{1,0:T(8,128)(2,1)}, u32[]{:S(2)}, u32[]{:S(2)}) collective-permute-start(bf16[640,1152]{1,0:T(8,128)(2,1)S(1)} %add_convert_fusion), channel_id=1, source_target_pairs={{0,2},{2,0},{1,3},{3,1},{4,6},{6,4},{5,7},{7,5},{8,10},{10,8},{9,1... | collective-permute-start | bytes 4423688 | tf_op jit(solution)/shard_map/ppermute | solution.py:200
  327.1 51.1 %collective-permute-start.10 = (bf16[640,1152]{1,0:T(8,128)(2,1)S(1)}, bf16[640,1152]{1,0:T(8,128)(2,1)S(1)}, u32[]{:S(2)}, u32[]{:S(2)}) collective-permute-start(bf16[640,1152]{1,0:T(8,128)(2,1)S(1)} %constant_dynamic-slice_fusion.10), channel_id=1, source_target_pairs={{0,1},{1,0},{2,3},{3,2},{4,5},{5,4},{6,7},{7,6},{8,9},{9,8},{10,11... | collective-permute-start | bytes 4423688 | tf_op jit(solution)/shard_map/ppermute | solution.py:181
  329.2 101.4 %collective-permute-start.21 = (bf16[512,1280]{1,0:T(8,128)(2,1)}, bf16[512,1280]{1,0:T(8,128)(2,1)S(1)}, u32[]{:S(2)}, u32[]{:S(2)}) collective-permute-start(bf16[512,1280]{1,0:T(8,128)(2,1)} %get-tuple-element.108), channel_id=1, source_target_pairs={{0,4},{28,24},{1,5},{29,25},{2,6},{30,26},{3,7},{31,27}} | collective-permute-start | bytes 3932168 | tf_op jit(solution)/shard_map/ppermute | solution.py:226
  378.2 52.9 %collective-permute-start.24 = (bf16[512,1280]{1,0:T(8,128)(2,1)}, bf16[512,1280]{1,0:T(8,128)(2,1)}, u32[]{:S(2)}, u32[]{:S(2)}) collective-permute-start(bf16[512,1280]{1,0:T(8,128)(2,1)} %get-tuple-element.109), channel_id=1, source_target_pairs={{8,4},{4,0},{20,24},{24,28},{9,5},{5,1},{21,25},{25,29},{10,6},{6,... | collective-permute-start | bytes 3932168 | tf_op jit(solution)/shard_map/ppermute | solution.py:226
  399.3 47.9 %collective-permute-start.40 = (bf16[640,1152]{1,0:T(8,128)(2,1)S(1)}, bf16[640,1152]{1,0:T(8,128)(2,1)S(1)}, u32[]{:S(2)}, u32[]{:S(2)}) collective-permute-start(bf16[640,1152]{1,0:T(8,128)(2,1)S(1)} %copy-done.8), channel_id=1, source_target_pairs={{0,2},{2,0},{1,3},{3,1},{4,6},{6,4},{5,7},{7,5},{8,10},{10,8},{9,1... | collective-permute-start | bytes 4423688 | tf_op jit(solution)/shard_map/ppermute | solution.py:200
  430.6 69.3 %collective-permute-start.39 = (bf16[640,1152]{1,0:T(8,128)(2,1)}, bf16[640,1152]{1,0:T(8,128)(2,1)}, u32[]{:S(2)}, u32[]{:S(2)}) collective-permute-start(bf16[640,1152]{1,0:T(8,128)(2,1)} %get-tuple-element.102), channel_id=1, source_target_pairs={{0,1},{1,0},{2,3},{3,2},{4,5},{5,4},{6,7},{7,6},{8,9},{9,8},{10,11... | collective-permute-start | bytes 4423688 | tf_op jit(solution)/shard_map/ppermute | solution.py:181
  430.6 70.6 %collective-permute-start.44 = (bf16[640,1152]{1,0:T(8,128)(2,1)}, bf16[640,1152]{1,0:T(8,128)(2,1)}, u32[]{:S(2)}, u32[]{:S(2)}) collective-permute-start(bf16[640,1152]{1,0:T(8,128)(2,1)} %get-tuple-element.100), channel_id=1, source_target_pairs={{0,1},{1,0},{2,3},{3,2},{4,5},{5,4},{6,7},{7,6},{8,9},{9,8},{10,11... | collective-permute-start | bytes 4423688 | tf_op jit(solution)/shard_map/ppermute | solution.py:181
  431.1 63.4 %collective-permute-start.18 = (bf16[512,1280]{1,0:T(8,128)(2,1)}, bf16[512,1280]{1,0:T(8,128)(2,1)}, u32[]{:S(2)}, u32[]{:S(2)}) collective-permute-start(bf16[512,1280]{1,0:T(8,128)(2,1)} %get-tuple-element.95), channel_id=1, source_target_pairs={{0,4},{28,24},{1,5},{29,25},{2,6},{30,26},{3,7},{31,27}} | collective-permute-start | bytes 3932168 | tf_op jit(solution)/shard_map/ppermute | solution.py:226
  433.5 55.9 %collective-permute-start.26 = (bf16[512,1280]{1,0:T(8,128)(2,1)}, bf16[512,1280]{1,0:T(8,128)(2,1)}, u32[]{:S(2)}, u32[]{:S(2)}) collective-permute-start(bf16[512,1280]{1,0:T(8,128)(2,1)} %get-tuple-element.99), channel_id=1, source_target_pairs={{0,4},{28,24},{1,5},{29,25},{2,6},{30,26},{3,7},{31,27}} | collective-permute-start | bytes 3932168 | tf_op jit(solution)/shard_map/ppermute | solution.py:226
  448.3 57.5 %collective-permute-start.33 = (bf16[640,1152]{1,0:T(8,128)(2,1)}, bf16[640,1152]{1,0:T(8,128)(2,1)}, u32[]{:S(2)}, u32[]{:S(2)}) collective-permute-start(bf16[640,1152]{1,0:T(8,128)(2,1)} %get-tuple-element.104), channel_id=1, source_target_pairs={{0,1},{1,0},{2,3},{3,2},{4,5},{5,4},{6,7},{7,6},{8,9},{9,8},{10,11... | collective-permute-start | bytes 4423688 | tf_op jit(solution)/shard_map/ppermute | solution.py:181
  499.9 57.8 %collective-permute-start.16 = (bf16[512,1280]{1,0:T(8,128)(2,1)}, bf16[512,1280]{1,0:T(8,128)(2,1)}, u32[]{:S(2)}, u32[]{:S(2)}) collective-permute-start(bf16[512,1280]{1,0:T(8,128)(2,1)} %get-tuple-element.107), channel_id=1, source_target_pairs={{8,4},{4,0},{20,24},{24,28},{9,5},{5,1},{21,25},{25,29},{10,6},{6,... | collective-permute-start | bytes 3932168 | tf_op jit(solution)/shard_map/ppermute | solution.py:226
  501.2 64.9 %collective-permute-start.25 = (bf16[512,1280]{1,0:T(8,128)(2,1)}, bf16[512,1280]{1,0:T(8,128)(2,1)}, u32[]{:S(2)}, u32[]{:S(2)}) collective-permute-start(bf16[512,1280]{1,0:T(8,128)(2,1)} %get-tuple-element.98), channel_id=1, source_target_pairs={{12,8},{16,20},{13,9},{17,21},{14,10},{18,22},{15,11},{19,23}} | collective-permute-start | bytes 3932168 | tf_op jit(solution)/shard_map/ppermute | solution.py:226
  505.8 61.7 %collective-permute-start.19 = (bf16[512,1280]{1,0:T(8,128)(2,1)}, bf16[512,1280]{1,0:T(8,128)(2,1)}, u32[]{:S(2)}, u32[]{:S(2)}) collective-permute-start(bf16[512,1280]{1,0:T(8,128)(2,1)} %select_convert_fusion.2), channel_id=1, source_target_pairs={{0,4},{4,8},{28,24},{24,20},{1,5},{5,9},{29,25},{25,21},{2,6},{6,1... | collective-permute-start | bytes 3932168 | tf_op jit(solution)/shard_map/ppermute | solution.py:226
  524.3 47.2 %collective-permute-start.37 = (bf16[640,1152]{1,0:T(8,128)(2,1)}, bf16[640,1152]{1,0:T(8,128)(2,1)S(1)}, u32[]{:S(2)}, u32[]{:S(2)}) collective-permute-start(bf16[640,1152]{1,0:T(8,128)(2,1)} %get-tuple-element.71), channel_id=1, source_target_pairs={{0,2},{2,0},{1,3},{3,1},{4,6},{6,4},{5,7},{7,5},{8,10},{10,8},{9,1... | collective-permute-start | bytes 4423688 | tf_op jit(solution)/shard_map/ppermute | solution.py:211
  528.3 44.9 %collective-permute-start.36 = (bf16[640,1152]{1,0:T(8,128)(2,1)}, bf16[640,1152]{1,0:T(8,128)(2,1)}, u32[]{:S(2)}, u32[]{:S(2)}) collective-permute-start(bf16[640,1152]{1,0:T(8,128)(2,1)} %get-tuple-element.71), channel_id=1, source_target_pairs={{0,1},{1,0},{2,3},{3,2},{4,5},{5,4},{6,7},{7,6},{8,9},{9,8},{10,11... | collective-permute-start | bytes 4423688 | tf_op jit(solution)/shard_map/ppermute | solution.py:212
  567.5 65.3 %collective-permute-start.42 = (bf16[640,1152]{1,0:T(8,128)(2,1)}, bf16[640,1152]{1,0:T(8,128)(2,1)}, u32[]{:S(2)}, u32[]{:S(2)}) collective-permute-start(bf16[640,1152]{1,0:T(8,128)(2,1)} %get-tuple-element.75), channel_id=1, source_target_pairs={{0,2},{2,0},{1,3},{3,1},{4,6},{6,4},{5,7},{7,5},{8,10},{10,8},{9,1... | collective-permute-start | bytes 4423688 | tf_op jit(solution)/shard_map/ppermute | solution.py:211
  573.3 59.5 %collective-permute-start.20 = (bf16[512,1280]{1,0:T(8,128)(2,1)}, bf16[512,1280]{1,0:T(8,128)(2,1)}, u32[]{:S(2)}, u32[]{:S(2)}) collective-permute-start(bf16[512,1280]{1,0:T(8,128)(2,1)} %add_convert_fusion.7), channel_id=1, source_target_pairs={{4,8},{8,12},{24,20},{20,16},{5,9},{9,13},{25,21},{21,17},{6,10},{... | collective-permute-start | bytes 3932168 | tf_op jit(solution)/shard_map/ppermute | solution.py:226
  580.1 59.0 %collective-permute-start.38 = (bf16[640,1152]{1,0:T(8,128)(2,1)S(1)}, bf16[640,1152]{1,0:T(8,128)(2,1)}, u32[]{:S(2)}, u32[]{:S(2)}) collective-permute-start(bf16[640,1152]{1,0:T(8,128)(2,1)S(1)} %collective-permute-done.37), channel_id=1, source_target_pairs={{0,1},{1,0},{2,3},{3,2},{4,5},{5,4},{6,7},{7,6},{8,9},{9,8},{10,11... | collective-permute-start | bytes 4423688 | tf_op jit(solution)/shard_map/ppermute | solution.py:213
  586.0 68.7 %collective-permute-start.46 = (bf16[640,1152]{1,0:T(8,128)(2,1)}, bf16[640,1152]{1,0:T(8,128)(2,1)S(1)}, u32[]{:S(2)}, u32[]{:S(2)}) collective-permute-start(bf16[640,1152]{1,0:T(8,128)(2,1)} %get-tuple-element.79), channel_id=1, source_target_pairs={{0,1},{1,0},{2,3},{3,2},{4,5},{5,4},{6,7},{7,6},{8,9},{9,8},{10,11... | collective-permute-start | bytes 4423688 | tf_op jit(solution)/shard_map/ppermute | solution.py:212
  601.7 42.7 %collective-permute-start.41 = (bf16[640,1152]{1,0:T(8,128)(2,1)}, bf16[640,1152]{1,0:T(8,128)(2,1)}, u32[]{:S(2)}, u32[]{:S(2)}) collective-permute-start(bf16[640,1152]{1,0:T(8,128)(2,1)} %get-tuple-element.75), channel_id=1, source_target_pairs={{0,1},{1,0},{2,3},{3,2},{4,5},{5,4},{6,7},{7,6},{8,9},{9,8},{10,11... | collective-permute-start | bytes 4423688 | tf_op jit(solution)/shard_map/ppermute | solution.py:212
  (46 other events, 1057.2 us)
